TPU v7x, 32 devices: a whole 2x2x4 slice. The times are simulated.
32 devices in a mesh: row: 4 (over y, x), col: 2 (over core), layer: 4 (over z).
Axes of the slice: x: 2, y: 2, z: 4, core: 2. Of those that a mesh axis runs over, the one named last changes fastest.
Arguments:
- matrix: float32 [4096, 4096], P('row', 'col'), may hold values from -6 to 6
- pattern: int32 [128, 128], P('row', 'col'), may hold values 0 or 1
- keep: int32 [128, 128], P('row', 'col'), may hold values 0 or 1
Outputs:
- update: float32 [4096, 4096], P(('row', 'layer'), 'col')
All inputs are finite; a program needn't handle non-finite values. No bound on the sum of `pattern` or of `keep` on one device may be relied on, other than what follows from the above.
Results may differ from a plain program's by a relative error of at most 0.00005.
Values sent between devices are 32-bit elements; how exact they have to be, the bound alone decides.
A program may use at most 128 MiB of HBM per device.

v0:
```python
import jax
import jax.numpy as jnp
from jax import lax
from jax.sharding import PartitionSpec as P

BS = 32
NB = 128


def layer_rows(values, layers, level):
    count, width = values.shape
    shaped = values.reshape(count // (layers * BS), layers, BS, width)
    picked = lax.dynamic_index_in_dim(shaped, level, 1, keepdims=False)
    return picked.reshape(count // layers, width)


def local(matrix, pattern, keep):
    rows, cols = matrix.shape
    block_rows, block_cols = pattern.shape
    layers = lax.axis_size("layer")
    level = lax.axis_index("layer")
    sparse = (
        matrix.reshape(block_rows, BS, block_cols, BS)
        * pattern.astype(jnp.float32)[:, None, :, None]
    ).reshape(rows, cols)
    left_local = lax.dynamic_index_in_dim(
        sparse.reshape(rows, block_cols // layers, layers, BS), level, 2, keepdims=False
    )
    left_local = left_local.reshape(rows, block_cols // layers * BS)
    left_full = lax.all_gather(left_local, "col", axis=1, tiled=True)
    right_full = lax.all_gather(layer_rows(sparse, layers, level), "row", axis=0, tiled=True)
    partial_value = jnp.dot(
        left_full, right_full, preferred_element_type=jnp.float32, precision=lax.Precision.HIGHEST
    )
    keep_flags = keep.astype(jnp.float32)
    keep_mine = lax.dynamic_index_in_dim(
        keep_flags.reshape(block_rows // layers, layers, block_cols), level, 1, keepdims=False
    )
    square = lax.psum(partial_value, "layer")
    mine = layer_rows(square, layers, level)
    filtered = (
        mine.reshape(block_rows // layers, BS, block_cols, BS) * keep_mine[:, None, :, None]
    ).reshape(rows // layers, cols)
    filtered_full = lax.all_gather(filtered, "row", axis=0, tiled=True)
    share = rows // layers
    summed = lax.psum_scatter(
        jnp.dot(
            left_full,
            filtered_full,
            preferred_element_type=jnp.float32,
            precision=lax.Precision.HIGHEST,
        ),
        "layer",
        scatter_dimension=0,
        tiled=True,
    )
    own_rows = lax.dynamic_slice_in_dim(sparse, level * share, share, 0)
    factor = 0.72 / (NB * BS)
    return 1.5 * own_rows - 0.5 * factor * summed


def solution(mesh):
    placed = (P("row", "col"), P("row", "col"), P("row", "col"))
    return jax.shard_map(
        local, mesh=mesh, in_specs=placed, out_specs=P(("row", "layer"), "col"), check_vma=False
    )
```

profile of v0, /device:TPU:0, one launch (start us, length us, event | category | flops | bytes accessed | tf_op | source)
XLA Modules:
  0.0 727.2 jit_solution(3081529053856967968)
XLA Ops:
  6.5 0.0 all-gather.4.cloned.1.call-start
  6.5 0.7 convert_element_type.6
  7.3 9.3 %copy.4 = f32[1024,2048]{0,1:T(8,128)} copy(f32[1024,2048]{1,0:T(8,128)} %param.3) | data formatting | bytes 16777216 | tf_op args[0]
  16.5 0.1 copy.5
  16.6 0.3 mul.63
  16.9 0.5 mul.64
  17.4 0.1 constant_dynamic-slice_fusion.3
  17.5 3.3 dynamic-slice_multiply_fusion.1
  20.8 0.0 all-gather.4.cloned.1.call-update
  20.8 0.0 all-gather.6.cloned.1.call-start
  20.9 0.3 mul.67
  21.2 0.5 mul.68
  21.7 0.1 constant_dynamic-slice_fusion.2
  21.8 3.2 dynamic-slice_multiply_fusion
  25.0 0.0 all-gather.6.cloned.1.call-update
  25.0 0.0 all-reduce.2.cloned.1.call-start
  25.1 12.3 %all-gather.4.cloned.1.call-done = f32[1024,1024]{0,1:T(8,128)} async-done(((f32[1024,512]{0,1:T(8,128)}), f32[1024,1024]{0,1:T(8,128)}) %all-gather.4.cloned.1.call-update) | async-done | bytes 4194320 | tf_op jit(solution)/shard_map/all_gather | solution.py:30
  37.4 90.5 %all-gather.6.cloned.1.call-done = f32[1024,2048]{1,0:T(8,128)} async-done(((f32[256,2048]{1,0:T(8,128)}), f32[1024,2048]{1,0:T(8,128)}) %all-gather.6.cloned.1.call-update) | async-done | bytes 8388624 | tf_op jit(solution)/shard_map/all_gather | solution.py:31
  127.9 31.0 %fusion.2 = f32[1024,2048]{1,0:T(8,128)} fusion(f32[1024,1024]{0,1:T(8,128)} %all-gather.4.cloned.1.call-done, f32[1024,2048]{1,0:T(8,128)} %all-gather.6.cloned.1.call-done), kind=kOutput, calls=%fused_computation.10 | convolution fusion | flops 25769803776 | bytes 20971520 | tf_op jit(solution)/shard_map/dot_general | solution.py:32
  158.9 0.0 copy-start
  158.9 0.0 all-reduce.2.cloned.1.call-update
  159.0 0.0 all-gather.8.cloned.1.call-start
  159.0 0.6 copy-done
  159.7 4.4 mul.72
  164.0 6.9 mul.73
  170.9 279.0 %all-reduce.2.cloned.1.call-done = f32[8,4,32,2048]{3,2,1,0:T(8,128)} async-done(((f32[8,4,32,2048]{3,2,1,0:T(8,128)}), f32[8,4,32,2048]{3,2,1,0:T(8,128)}) %all-reduce.2.cloned.1.call-update) | async-done | bytes 8388624 | tf_op jit(solution)/shard_map/psum | solution.py:39
  449.9 1.7 constant_dynamic-slice_fusion.1
  451.7 1.6 bitcast_multiply_fusion
  453.3 0.0 all-gather.8.cloned.1.call-update
  453.3 0.2 reduce-scatter.2.cloned.1.call-start
  453.5 86.4 %all-gather.8.cloned.1.call-done = f32[1024,2048]{1,0:T(8,128)} async-done(((f32[256,2048]{1,0:T(8,128)}), f32[1024,2048]{1,0:T(8,128)}) %all-gather.8.cloned.1.call-update) | async-done | bytes 8388624 | tf_op jit(solution)/shard_map/all_gather | solution.py:44
  539.9 31.0 %fusion.3 = f32[1024,2048]{1,0:T(8,128)} fusion(f32[1024,1024]{0,1:T(8,128)} %all-gather.4.cloned.1.call-done, f32[1024,2048]{1,0:T(8,128)} %all-gather.8.cloned.1.call-done), kind=kOutput, calls=%fused_computation.11 | convolution fusion | flops 25769803776 | bytes 20971520 | tf_op jit(solution)/shard_map/dot_general | solution.py:47
  571.0 0.0 reduce-scatter.2.cloned.1.call-update
  571.0 11.7 %mul.57 = f32[32,32,64,32]{3,2,1,0:T(8,128)} broadcast(f32[32,64]{1,0:T(8,128)S(1)} %convert_element_type.6), dimensions={0,2} | broadcast | bytes 8396800 | tf_op jit(solution)/shard_map/mul | solution.py:23
  582.6 25.5 %mul.58 = f32[1024,2048]{1,0:T(8,128)} reshape(f32[32,32,64,32]{3,2,1,0:T(8,128)} %mul.57) | data formatting | bytes 16777216 | tf_op jit(solution)/shard_map/mul | solution.py:23
  608.1 107.7 %reduce-scatter.2.cloned.1.call-done = f32[256,2048]{1,0:T(8,128)} async-done(((f32[1024,2048]{1,0:T(8,128)}), f32[256,2048]{1,0:T(8,128)}) %reduce-scatter.2.cloned.1.call-update) | async-done | bytes 2097168 | tf_op jit(solution)/shard_map/reduce_scatter | solution.py:46
  715.7 5.0 fusion.1
  (2 shorter events, 0.0 us)
Async XLA Ops:
  6.5 30.8 %all-gather.4.cloned.1.call-start = ((), (), s32[]{:S(2)}) async-start(), calls=%async_computation.1 | async-start | bytes 6291456 | tf_op jit(solution)/shard_map/all_gather | solution.py:30
  20.8 107.1 %all-gather.6.cloned.1.call-start = ((), (), s32[]{:S(2)}) async-start(), calls=%async_computation.2 | async-start | bytes 10485760 | tf_op jit(solution)/shard_map/all_gather | solution.py:31
  25.0 424.9 %all-reduce.2.cloned.1.call-start = ((), (), s32[]{:S(2)}) async-start(), calls=%async_computation.3 | async-start | bytes 16777216 | tf_op jit(solution)/shard_map/psum | solution.py:39
  158.9 0.7 copy-start
  159.0 381.0 %all-gather.8.cloned.1.call-start = ((), (), s32[]{:S(2)}) async-start(), calls=%async_computation.4 | async-start | bytes 10485760 | tf_op jit(solution)/shard_map/all_gather | solution.py:44
  453.3 262.4 %reduce-scatter.2.cloned.1.call-start = ((), (), s32[]{:S(2)}) async-start(), calls=%async_computation.5 | async-start | bytes 10485760 | tf_op jit(solution)/shard_map/reduce_scatter | solution.py:46
Sparse Core Ops, SparseCore 0:
  20.9 16.3 all-gather.3
  39.2 88.6 all-gather.5
  159.1 290.8 all-reduce.1
  453.4 86.4 all-gather.7
  571.1 144.6 reduce-scatter.1
where the time goes:
time: 728 us; the launch traced here: 727 us
  waiting for transfers between devices  576 us (79%)
  matrix products  62.1 us (9%)
  local copies, waits for them, and re-layouts  61.9 us (9%)
  other arithmetic  13.8 us (2%)
  between operations  13.2 us (2%)
    psum x1, waiting for transfers between devices, local(): square = lax.psum(partial_value, 'layer')  279 us
    reduce_scatter x1, waiting for transfers between devices, local(): lax.psum_scatter(jnp.dot(left_full, filtered_full, preferred_element_type...  108 us
    all_gather x1, waiting for transfers between devices, local(): lax.all_gather(layer_rows(sparse, layers, level), 'row', axis=0, tiled=True)  90.5 us
    all_gather x1, waiting for transfers between devices, local(): filtered_full = lax.all_gather(filtered, 'row', axis=0, tiled=True)  86.4 us
    mul x6, local copies, waits for them, and re-layouts, local(): matrix.reshape(block_rows, BS, block_cols, BS)  38.8 us
    dot_general x1, matrix products, local(): jnp.dot(left_full, right_full, preferred_element_type=jnp.float32, precis...  31 us
    dot_general x1, matrix products, local(): jnp.dot(left_full, filtered_full, preferred_element_type=jnp.float32, pre...  31 us
  transfers between devices with their start and end apart: 5, of which 5 were waited for; matrix products, arithmetic and copies ran while one was open for 7% of the time, Pallas kernels for 0%

commit v1 on v0

--- a/solution.py
+++ b/solution.py
@@ -36,7 +36,9 @@
     keep_mine = lax.dynamic_index_in_dim(
         keep_flags.reshape(block_rows // layers, layers, block_cols), level, 1, keepdims=False
     )
-    square = lax.psum(partial_value, "layer")
+    square = partial_value
+    for hop in (1, 2):
+        square = square + lax.ppermute(square, "layer", [(dev, dev ^ hop) for dev in range(4)])
     mine = layer_rows(square, layers, level)
     filtered = (
         mine.reshape(block_rows // layers, BS, block_cols, BS) * keep_mine[:, None, :, None]

time: 728 us -> 1010 us (1.39)
  waiting for transfers between devices: 576 us -> 827 us
  other arithmetic: 13.8 us -> 37.2 us
    ppermute x0 -> x2, waiting for transfers between devices: none -> 529 us  [local(): lax.ppermute(square, 'layer', [(dev, dev ^ hop) for dev in range(4)])]
    psum x1 -> x0, waiting for transfers between devices: 279 us -> none  [local(): square = lax.psum(partial_value, 'layer')]
    add x0 -> x2, other arithmetic: none -> 23.4 us  [local(): square + lax.ppermute(square, 'layer', [(dev, dev ^ hop) for dev in range...]
  transfers between devices with their start and end apart: 5 -> 6, of which waited for: 5 -> 6; matrix products, arithmetic and copies ran while one was open for 7% -> 5% of each run, Pallas kernels for 0% -> 0%
where the time goes in v1:
time: 1010 us
  waiting for transfers between devices  827 us (82%)
  local copies, waits for them, and re-layouts  64.2 us (6%)
  matrix products  60.7 us (6%)
  other arithmetic  37.2 us (4%)
  between operations  13.2 us (1%)
    ppermute x2, waiting for transfers between devices, local(): lax.ppermute(square, 'layer', [(dev, dev ^ hop) for dev in range(4)])  529 us
    reduce_scatter x1, waiting for transfers between devices, local(): lax.psum_scatter(jnp.dot(left_full, filtered_full, preferred_element_type...  108 us
    all_gather x1, waiting for transfers between devices, local(): lax.all_gather(layer_rows(sparse, layers, level), 'row', axis=0, tiled=True)  90.5 us
    all_gather x1, waiting for transfers between devices, local(): filtered_full = lax.all_gather(filtered, 'row', axis=0, tiled=True)  87.6 us
    mul x6, local copies, waits for them, and re-layouts, local(): matrix.reshape(block_rows, BS, block_cols, BS)  38.7 us
    dot_general x1, matrix products, local(): jnp.dot(left_full, filtered_full, preferred_element_type=jnp.float32, pre...  31 us
    dot_general x1, matrix products, local(): jnp.dot(left_full, right_full, preferred_element_type=jnp.float32, precis...  29.7 us
    add x2, other arithmetic, local(): square + lax.ppermute(square, 'layer', [(dev, dev ^ hop) for dev in range...  23.4 us
  transfers between devices with their start and end apart: 6, of which 6 were waited for; matrix products, arithmetic and copies ran while one was open for 5% of the time, Pallas kernels for 0%

profile of v1, /device:TPU:0, one launch (start us, length us, event | category | flops | bytes accessed | tf_op | source)
XLA Modules:
  0.0 1006.8 jit_solution(2441784847759672998)
XLA Ops:
  6.5 0.0 all-gather.4.cloned.1.call-start
  6.5 0.7 convert_element_type.6
  7.3 9.3 copy.4
  16.5 0.1 copy.5
  16.6 0.3 mul.63
  16.9 0.5 mul.64
  17.4 0.1 constant_dynamic-slice_fusion.3
  17.5 3.3 dynamic-slice_multiply_fusion.1
  20.8 0.0 all-gather.4.cloned.1.call-update
  20.8 0.0 all-gather.6.cloned.1.call-start
  20.9 0.3 mul.67
  21.2 0.5 mul.68
  21.7 0.1 constant_dynamic-slice_fusion.2
  21.8 3.3 dynamic-slice_multiply_fusion
  25.0 0.0 all-gather.6.cloned.1.call-update
  25.1 0.2 all-gather.8.cloned.1.call-start
  25.3 12.1 %all-gather.4.cloned.1.call-done = f32[1024,1024]{0,1:T(8,128)} async-done(((f32[1024,512]{0,1:T(8,128)}), f32[1024,1024]{0,1:T(8,128)}) %all-gather.4.cloned.1.call-update) | async-done | bytes 4194320 | tf_op jit(solution)/shard_map/all_gather | solution.py:30
  37.4 90.5 %all-gather.6.cloned.1.call-done = f32[1024,2048]{1,0:T(8,128)} async-done(((f32[256,2048]{1,0:T(8,128)}), f32[1024,2048]{1,0:T(8,128)}) %all-gather.6.cloned.1.call-update) | async-done | bytes 8388624 | tf_op jit(solution)/shard_map/all_gather | solution.py:31
  127.9 29.7 %fusion.2 = f32[1024,2048]{1,0:T(8,128)S(1)} fusion(f32[1024,1024]{0,1:T(8,128)} %all-gather.4.cloned.1.call-done, f32[1024,2048]{1,0:T(8,128)} %all-gather.6.cloned.1.call-done), kind=kOutput, calls=%fused_computation.10 | convolution fusion | flops 25769803776 | bytes 20971520 | tf_op jit(solution)/shard_map/dot_general | solution.py:32
  157.6 0.0 copy-start
  157.6 3.2 copy-done
  160.8 0.0 copy-start.1
  160.8 1.5 collective-permute-start
  162.3 180.7 %collective-permute-done = f32[1024,2048]{1,0:T(8,128)} collective-permute-done((f32[1024,2048]{1,0:T(8,128)S(1)}, f32[1024,2048]{1,0:T(8,128)}, u32[]{:S(2)}, u32[]{:S(2)}) %collective-permute-start) | collective-permute-done | bytes 8388640 | tf_op jit(solution)/shard_map/ppermute | solution.py:41
  342.9 11.7 %add.22 = f32[1024,2048]{1,0:T(8,128)} add(f32[1024,2048]{1,0:T(8,128)} %copy-done, f32[1024,2048]{1,0:T(8,128)} %collective-permute-done) | non-fusion elementwise | flops 2097152 | bytes 25165824 | tf_op jit(solution)/shard_map/add | solution.py:41
  354.6 2.4 collective-permute-start.1
  357.0 0.0 copy-done.1
  357.1 4.4 mul.72
  361.4 6.7 mul.73
  368.1 348.7 %collective-permute-done.1 = f32[1024,2048]{1,0:T(8,128)} collective-permute-done((f32[1024,2048]{1,0:T(8,128)}, f32[1024,2048]{1,0:T(8,128)}, u32[]{:S(2)}, u32[]{:S(2)}) %collective-permute-start.1) | collective-permute-done | bytes 8388640 | tf_op jit(solution)/shard_map/ppermute | solution.py:41
  716.8 11.7 %add.23 = f32[1024,2048]{1,0:T(8,128)} add(f32[1024,2048]{1,0:T(8,128)} %add.22, f32[1024,2048]{1,0:T(8,128)} %collective-permute-done.1) | non-fusion elementwise | flops 2097152 | bytes 25165824 | tf_op jit(solution)/shard_map/add | solution.py:41
  728.5 1.7 constant_dynamic-slice_fusion.1
  730.2 1.6 bitcast_multiply_fusion
  731.9 0.0 all-gather.8.cloned.1.call-update
  731.9 0.0 reduce-scatter.2.cloned.1.call-start
  731.9 87.6 %all-gather.8.cloned.1.call-done = f32[1024,2048]{1,0:T(8,128)} async-done(((f32[256,2048]{1,0:T(8,128)}), f32[1024,2048]{1,0:T(8,128)}) %all-gather.8.cloned.1.call-update) | async-done | bytes 8388624 | tf_op jit(solution)/shard_map/all_gather | solution.py:46
  819.5 31.0 %fusion.3 = f32[1024,2048]{1,0:T(8,128)} fusion(f32[1024,1024]{0,1:T(8,128)} %all-gather.4.cloned.1.call-done, f32[1024,2048]{1,0:T(8,128)} %all-gather.8.cloned.1.call-done), kind=kOutput, calls=%fused_computation.11 | convolution fusion | flops 25769803776 | bytes 20971520 | tf_op jit(solution)/shard_map/dot_general | solution.py:49
  850.5 0.0 reduce-scatter.2.cloned.1.call-update
  850.5 11.7 %mul.57 = f32[32,32,64,32]{3,2,1,0:T(8,128)} broadcast(f32[32,64]{1,0:T(8,128)S(1)} %convert_element_type.6), dimensions={0,2} | broadcast | bytes 8396800 | tf_op jit(solution)/shard_map/mul | solution.py:23
  862.2 25.4 %mul.58 = f32[1024,2048]{1,0:T(8,128)} reshape(f32[32,32,64,32]{3,2,1,0:T(8,128)} %mul.57) | data formatting | bytes 16777216 | tf_op jit(solution)/shard_map/mul | solution.py:23
  887.6 107.7 %reduce-scatter.2.cloned.1.call-done = f32[256,2048]{1,0:T(8,128)} async-done(((f32[1024,2048]{1,0:T(8,128)}), f32[256,2048]{1,0:T(8,128)}) %reduce-scatter.2.cloned.1.call-update) | async-done | bytes 2097168 | tf_op jit(solution)/shard_map/reduce_scatter | solution.py:48
  995.3 5.0 fusion.1
  (2 shorter events, 0.0 us)
Async XLA Ops:
  6.5 30.8 %all-gather.4.cloned.1.call-start = ((), (), s32[]{:S(2)}) async-start(), calls=%async_computation.1 | async-start | bytes 6291456 | tf_op jit(solution)/shard_map/all_gather | solution.py:30
  20.8 107.1 %all-gather.6.cloned.1.call-start = ((), (), s32[]{:S(2)}) async-start(), calls=%async_computation.2 | async-start | bytes 10485760 | tf_op jit(solution)/shard_map/all_gather | solution.py:31
  25.1 794.4 %all-gather.8.cloned.1.call-start = ((), (), s32[]{:S(2)}) async-start(), calls=%async_computation.3 | async-start | bytes 10485760 | tf_op jit(solution)/shard_map/all_gather | solution.py:46
  157.6 3.2 copy-start
  160.8 196.2 %copy-start.1 = (s32[32,64]{1,0:T(8,128)S(1)}, s32[32,64]{1,0:T(8,128)}, u32[]{:S(2)}) copy-start(s32[32,64]{1,0:T(8,128)} %param.5) | copy-start | bytes 24580
  160.8 182.1 %collective-permute-start = (f32[1024,2048]{1,0:T(8,128)S(1)}, f32[1024,2048]{1,0:T(8,128)}, u32[]{:S(2)}, u32[]{:S(2)}) collective-permute-start(f32[1024,2048]{1,0:T(8,128)S(1)} %fusion.2), channel_id=1, source_target_pairs={{0,1},{1,0},{2,3},{3,2},{4,5},{5,4},{6,7},{7,6},{8,9},{9,8},{10,11... | collective-permute-start | bytes 25165832 | tf_op jit(solution)/shard_map/ppermute | solution.py:41
  354.6 362.1 %collective-permute-start.1 = (f32[1024,2048]{1,0:T(8,128)}, f32[1024,2048]{1,0:T(8,128)}, u32[]{:S(2)}, u32[]{:S(2)}) collective-permute-start(f32[1024,2048]{1,0:T(8,128)} %add.22), channel_id=1, source_target_pairs={{0,2},{1,3},{2,0},{3,1},{4,6},{5,7},{6,4},{7,5},{8,10},{9,11},{10,... | collective-permute-start | bytes 25165832 | tf_op jit(solution)/shard_map/ppermute | solution.py:41
  731.9 263.4 %reduce-scatter.2.cloned.1.call-start = ((), (), s32[]{:S(2)}) async-start(), calls=%async_computation.4 | async-start | bytes 10485760 | tf_op jit(solution)/shard_map/reduce_scatter | solution.py:48
Sparse Core Ops, SparseCore 0:
  20.9 16.3 all-gather.3
  39.2 88.6 all-gather.5
  732.0 87.4 all-gather.7
  850.7 144.6 reduce-scatter.1
